TPU v7x, 32 devices: a whole 2x2x4 slice. The times are simulated.
32 devices in a mesh: seq: 8 (over z, x), res: 4 (over y, core).
Axes of the slice: x: 2, y: 2, z: 4, core: 2. Of those that a mesh axis runs over, the one named last changes fastest.
Arguments:
- alignment: bfloat16 [128, 4, 128, 256], P('seq', 'res'), may hold values from -8 to 8
- gain_attn: float32 [256], replicated, may hold values from 0.1 to 1.9
- w_proj: bfloat16 [256, 4, 256], replicated, may hold values from -0.75 to 0.75
- w_out: bfloat16 [256, 256], replicated, may hold values from -0.375 to 0.375
- gain_head: float32 [256], replicated, may hold values from 0.1 to 1.9
- w_head: bfloat16 [256, 23], replicated, may hold values from -1 to 1
- masked: int32 [128, 4, 128], P('res', None, 'seq'), may hold values from 0 to 1
- labels: int32 [128, 4, 128], P('res', None, 'seq'), may hold values from 0 to 22
Outputs:
- updated: bfloat16 [128, 4, 128, 256], P('res', None, 'seq')
- masked_loss: float32 [], replicated
- mask_share: float32 [], replicated
All inputs are finite; a program needn't handle non-finite values.
Results may differ from a plain program's by a relative error of at most 0.011.
Values may be sent and summed in bfloat16 or wider, within the bound.
A program may use at most 192 MiB of HBM per device.

v0:
```python
import jax
import jax.numpy as jnp
from jax import lax
from jax.sharding import PartitionSpec as P

HEADS = 8
HEAD_DIM = 32


def normalize(values, gain):
    mean = jnp.mean(values, axis=-1, keepdims=True)
    centred = values - mean
    spread = jnp.mean(centred * centred, axis=-1, keepdims=True)
    return centred * lax.rsqrt(spread + 1e-05) * gain


def project(flat_rows, gain_attn, w_proj):
    features = flat_rows.shape[1]
    normed = normalize(flat_rows.astype(jnp.float32), gain_attn).astype(jnp.bfloat16)
    return jnp.dot(
        normed, w_proj.reshape(features, 4 * features), preferred_element_type=jnp.float32
    ).astype(jnp.bfloat16)


def column_attention(queries, key_part, value_part):
    inv_root = HEAD_DIM ** (-0.5)
    scores = (
        jnp.einsum("shd,thd->hst", queries, key_part, preferred_element_type=jnp.float32) * inv_root
    )
    probs = jnp.exp(scores)
    totals = jnp.sum(probs, axis=2)
    weighted = jnp.einsum(
        "hst,thd->shd", probs.astype(jnp.bfloat16), value_part, preferred_element_type=jnp.float32
    )
    return (weighted, totals)


def finish(flat_rows, gated, w_out):
    summed = flat_rows.astype(jnp.float32) + jnp.dot(
        gated, w_out, preferred_element_type=jnp.float32
    )
    return summed.astype(jnp.bfloat16)


def on_device(alignment, gain_attn, w_proj, w_out, gain_head, w_head, masked, labels):
    weights = masked.reshape(-1).astype(jnp.float32)
    local_count = jnp.sum(weights)
    local_rows, single_block, segment, features = alignment.shape
    seq_devices = lax.axis_size("seq")
    split_view = alignment.reshape(local_rows, seq_devices, segment // seq_devices, features)
    column_block = lax.all_to_all(split_view, "seq", split_axis=1, concat_axis=0, tiled=True)
    seq_total, single, col_count, features = column_block.shape
    by_column = jnp.transpose(column_block.reshape(seq_total, col_count, features), (1, 0, 2))
    flat_rows = by_column.reshape(col_count * seq_total, features)
    projected = project(flat_rows, gain_attn, w_proj).reshape(
        col_count, seq_total, 4, HEADS, HEAD_DIM
    )

    def per_column(picked):
        weighted, totals = column_attention(picked[:, 0], picked[:, 1], picked[:, 2])
        attended = weighted / totals.T[:, :, None]
        gated_col = attended * jax.nn.sigmoid(picked[:, 3].astype(jnp.float32))
        return gated_col.reshape(seq_total, features).astype(jnp.bfloat16)

    gated = lax.map(per_column, projected).reshape(col_count * seq_total, features)
    result = finish(flat_rows, gated, w_out).reshape(col_count, seq_total, features)
    result = jnp.transpose(result, (1, 0, 2)).reshape(seq_total, single, col_count, features)
    updated = lax.all_to_all(result, "res", split_axis=0, concat_axis=1, tiled=True)
    features = updated.shape[3]
    flat_out = updated.reshape(-1, features)
    head_in = normalize(flat_out.astype(jnp.float32), gain_head).astype(jnp.bfloat16)
    logits = jnp.einsum("rc,ck->kr", head_in, w_head, preferred_element_type=jnp.float32)
    log_total = jnp.log(jnp.sum(jnp.exp(logits), axis=0))
    classes = jnp.arange(logits.shape[0], dtype=jnp.int32)[:, None]
    picked = jnp.sum(jnp.where(classes == labels.reshape(1, -1), logits, 0.0), axis=0)
    errors = log_total - picked
    local_loss = jnp.sum(errors * weights)
    loss_sum, mask_count = lax.psum((local_loss, local_count), ("seq", "res"))
    entries = flat_out.shape[0] * lax.axis_size("seq") * lax.axis_size("res")
    masked_loss = loss_sum / (1.0 + mask_count)
    mask_share = mask_count / entries
    return (updated, masked_loss, mask_share)


def solution(mesh):
    in_specs = (
        P("seq", "res", None, None),
        P(),
        P(),
        P(),
        P(),
        P(),
        P("res", None, "seq"),
        P("res", None, "seq"),
    )
    out_specs = (P("res", None, "seq", None), P(), P())
    return jax.shard_map(
        on_device, mesh=mesh, in_specs=in_specs, out_specs=out_specs, check_vma=False
    )
```

profile of v0, /device:TPU:12, one launch (start us, length us, event | category | flops | bytes accessed | tf_op | source)
XLA Modules:
  0.0 152.1 jit_solution(10787070603162363327)
XLA Ops:
  0.7 2.4 %copy.61 = bf16[16,8,16,256]{3,2,0,1:T(8,128)(2,1)} copy(bf16[16,8,16,256]{3,2,1,0:T(8,128)(2,1)} %bitcast.113) | data formatting | bytes 2097152 | tf_op jit(solution)/shard_map/reshape | solution.py:50
  3.0 6.3 %all-to-all-start = ((bf16[16,8,16,256]{3,2,0,1:T(8,128)(2,1)}), bf16[16,8,16,256]{3,2,0,1:T(8,128)(2,1)S(1)}, u32[]{:S(2)}, u32[]{:S(2)}) async-start(bf16[16,8,16,256]{3,2,0,1:T(8,128)(2,1)} %copy.61), calls=%async_computation | async-start | bytes 2097152 | tf_op jit(solution)/shard_map/all_to_all | solution.py:51
  9.4 23.3 %all-to-all-done = bf16[16,8,16,256]{3,2,0,1:T(8,128)(2,1)S(1)} async-done(((bf16[16,8,16,256]{3,2,0,1:T(8,128)(2,1)}), bf16[16,8,16,256]{3,2,0,1:T(8,128)(2,1)S(1)}, u32[]{:S(2)}, u32[]{:S(2)}) %all-to-all-start) | async-done | bytes 1048608 | tf_op jit(solution)/shard_map/all_to_all | solution.py:51
  32.9 1.2 bitcast_reduce_fusion
  34.1 1.2 copy.62
  35.3 1.6 %multiply_reduce_fusion.1 = f32[16,128]{1,0:T(8,128)S(1)} fusion(f32[16,128]{1,0:T(8,128)S(1)} %broadcast_multiply_fusion.1, f32[128,16,256]{2,1,0:T(8,128)S(1)} %bitcast.100), kind=kLoop, calls=%fused_computation.24 | loop fusion | flops 1570816 | bytes 2113536 | tf_op jit(solution)/shard_map/reduce_sum | solution.py:13
  37.0 1.4 multiply_convert_fusion
  38.3 3.2 %convolution_convert_fusion = bf16[2048,1024]{1,0:T(8,128)(2,1)} fusion(bf16[2048,256]{1,0:T(8,128)(2,1)S(1)} %bitcast.109, bf16[256,1024]{1,0:T(8,128)(2,1)S(1)} %bitcast.111), kind=kOutput, calls=%fused_computation.12 | convolution fusion | flops 1075838976 | bytes 5767168 | tf_op jit(solution)/shard_map/dot_general | solution.py:20
  41.5 6.5 %copy.63 = bf16[2048,1024]{0,1:T(8,128)(2,1)} copy(bf16[2048,1024]{1,0:T(8,128)(2,1)} %convolution_convert_fusion) | data formatting | bytes 8388608 | tf_op jit(solution)/shard_map/convert_element_type | solution.py:22
  48.0 3.6 %copy.80 = bf16[128,8,16,128]{3,2,1,0:T(8,128)(2,1)S(1)} copy(bf16[128,8,16,128]{3,1,2,0:T(8,128)(2,1)} %bitcast.106) | data formatting | bytes 8388608
  51.6 3.0 %copy.64 = bf16[16,128,4,8,32]{1,4,3,2,0:T(8,128)(2,1)} copy(bf16[16,128,4,8,32]{1,0,4,3,2:T(8,128)(2,1)S(1)} %bitcast.107) | data formatting | bytes 8388608 | tf_op jit(solution)/shard_map/while | solution.py:65
  54.7 26.1 %while.10 = (s32[]{:T(128)}, bf16[16,128,256]{2,1,0:T(8,128)(2,1)S(1)}, bf16[16,128,4,8,32]{1,4,3,2,0:T(8,128)(2,1)}, s32[]{:T(128)}) while((s32[]{:T(128)}, bf16[16,128,256]{2,1,0:T(8,128)(2,1)S(1)}, bf16[16,128,4,8,32]{1,4,3,2,0:T(8,128)(2,1)}, s32[]{:T(128)}) %tuple.42), condition=%wide.region_4.0_spmd, body=%wide.region_2.4_spmd.sunk | while | flops 17398784 | bytes 1646653 | solution.py:65
  56.3 1.0 dynamic-slice_bitcast_fusion.2
  57.9 1.0 dynamic-slice_bitcast_fusion.2
  59.6 1.0 dynamic-slice_bitcast_fusion.2
  61.2 1.0 dynamic-slice_bitcast_fusion.2
  62.8 1.0 dynamic-slice_bitcast_fusion.2
  64.5 1.0 dynamic-slice_bitcast_fusion.2
  66.1 1.0 dynamic-slice_bitcast_fusion.2
  67.7 1.0 dynamic-slice_bitcast_fusion.2
  69.4 1.0 dynamic-slice_bitcast_fusion.2
  71.0 1.0 dynamic-slice_bitcast_fusion.2
  72.6 1.0 dynamic-slice_bitcast_fusion.2
  74.3 1.0 dynamic-slice_bitcast_fusion.2
  75.9 1.0 dynamic-slice_bitcast_fusion.2
  77.5 1.0 dynamic-slice_bitcast_fusion.2
  81.3 1.6 %copy.85 = bf16[16,128,256]{2,0,1:T(8,128)(2,1)} copy(bf16[16,128,256]{2,1,0:T(8,128)(2,1)S(1)} %bitcast.110) | data formatting | bytes 2097152 | tf_op jit(solution)/shard_map/reshape | solution.py:66
  82.8 4.0 %all-to-all-start.1 = ((bf16[128,1,16,256]{3,2,1,0:T(8,128)(2,1)}), bf16[128,1,16,256]{3,2,1,0:T(8,128)(2,1)S(1)}, u32[]{:S(2)}, u32[]{:S(2)}) async-start(bf16[128,1,16,256]{3,2,1,0:T(8,128)(2,1)} %bitcast.79), calls=%async_computation.1 | async-start | bytes 2097152 | tf_op jit(solution)/shard_map/all_to_all | solution.py:68
  87.1 12.5 %all-to-all-done.1 = bf16[128,1,16,256]{3,2,1,0:T(8,128)(2,1)S(1)} async-done(((bf16[128,1,16,256]{3,2,1,0:T(8,128)(2,1)}), bf16[128,1,16,256]{3,2,1,0:T(8,128)(2,1)S(1)}, u32[]{:S(2)}, u32[]{:S(2)}) %all-to-all-start.1) | async-done | bytes 1048608 | tf_op jit(solution)/shard_map/all_to_all | solution.py:68
  102.5 1.1 exponential_reduce_fusion
  104.4 42.4 %all-reduce = (f32[]{:T(128)}, f32[]{:T(128)}) all-reduce(f32[]{:T(128)} %get-tuple-element.57, f32[]{:T(128)} %get-tuple-element.56), channel_id=1, replica_groups=mesh['seq'=8,'res'=4] {'seq','res'}, use_global_device_ids=true, to_apply=%region_10.11 | all-reduce | flops 2 | bytes 16 | tf_op jit(solution)/shard_map/psum | solution.py:78
  148.1 1.1 copy.75
  (105 shorter events, 16.6 us)
Async XLA Ops:
  0.6 80.2 %copy-start = (bf16[256,256]{1,0:T(8,128)(2,1)S(1)}, bf16[256,256]{1,0:T(8,128)(2,1)}, u32[]{:S(2)}) copy-start(bf16[256,256]{1,0:T(8,128)(2,1)} %param.13) | copy-start | bytes 393220
  0.6 8.6 %copy-start.2 = (bf16[256,4,256]{2,1,0:T(4,128)(2,1)S(1)}, bf16[256,4,256]{2,1,0:T(4,128)(2,1)}, u32[]{:S(2)}) copy-start(bf16[256,4,256]{2,1,0:T(4,128)(2,1)} %param.12) | copy-start | bytes 1572868
  3.0 29.6 %all-to-all-start = ((bf16[16,8,16,256]{3,2,0,1:T(8,128)(2,1)}), bf16[16,8,16,256]{3,2,0,1:T(8,128)(2,1)S(1)}, u32[]{:S(2)}, u32[]{:S(2)}) async-start(bf16[16,8,16,256]{3,2,0,1:T(8,128)(2,1)} %copy.61), calls=%async_computation | async-start | bytes 2097152 | tf_op jit(solution)/shard_map/all_to_all | solution.py:51
  35.3 1.7 %copy-start.5 = (f32[256]{0:T(256)S(1)}, f32[256]{0:T(256)}, u32[]{:S(2)}) copy-start(f32[256]{0:T(256)} %param.11) | copy-start | bytes 3076
  51.6 3.0 %copy-start.1 = (bf16[16,128,256]{2,1,0:T(8,128)(2,1)S(1)}, bf16[16,128,256]{2,1,0:T(8,128)(2,1)}, u32[]{:S(2)}) copy-start(bf16[16,128,256]{2,1,0:T(8,128)(2,1)} %custom-call) | copy-start | bytes 3145732
  81.3 5.6 %copy-start.3 = (s32[32,4,16]{0,2,1:T(8,128)S(1)}, s32[32,4,16]{0,2,1:T(8,128)}, u32[]{:S(2)}) copy-start(s32[32,4,16]{0,2,1:T(8,128)} %param.17) | copy-start | bytes 24580
  81.3 5.7 %copy-start.4 = (s32[32,4,16]{0,2,1:T(8,128)S(1)}, s32[32,4,16]{0,2,1:T(8,128)}, u32[]{:S(2)}) copy-start(s32[32,4,16]{0,2,1:T(8,128)} %param.16) | copy-start | bytes 24580
  82.8 16.8 %all-to-all-start.1 = ((bf16[128,1,16,256]{3,2,1,0:T(8,128)(2,1)}), bf16[128,1,16,256]{3,2,1,0:T(8,128)(2,1)S(1)}, u32[]{:S(2)}, u32[]{:S(2)}) async-start(bf16[128,1,16,256]{3,2,1,0:T(8,128)(2,1)} %bitcast.79), calls=%async_computation.1 | async-start | bytes 2097152 | tf_op jit(solution)/shard_map/all_to_all | solution.py:68
  100.2 1.4 copy-start.6
where the time goes:
time: 153 us; the launch traced here: 152 us
  blocking collectives  42.4 us (28%)
  local copies, waits for them, and re-layouts  38.2 us (25%)
  waiting for transfers between devices  35.8 us (23%)
  matrix products  12.7 us (8%)
  starting transfers between devices  10.2 us (7%)
  other arithmetic  7 us (5%)
  between operations  5.09 us (3%)
    psum x1, blocking collectives, on_device(): loss_sum, mask_count = lax.psum((local_loss, local_count), ('seq', 'res'))  42.4 us
    all_to_all x1, waiting for transfers between devices, on_device(): lax.all_to_all(split_view, 'seq', split_axis=1, concat_axis=0, tiled=True)  23.3 us
    squeeze x16, local copies, waits for them, and re-layouts, on_device(): lax.map(per_column, projected).reshape(col_count * seq_total, features)  15.5 us
    all_to_all x1, waiting for transfers between devices, on_device(): lax.all_to_all(result, 'res', split_axis=0, concat_axis=1, tiled=True)  12.5 us
    convert_element_type x1, local copies, waits for them, and re-layouts, project(): return jnp.dot(normed, w_proj.reshape(features, 4 * features), preferred_...  6.52 us
    all_to_all x1, starting transfers between devices, on_device(): lax.all_to_all(split_view, 'seq', split_axis=1, concat_axis=0, tiled=True)  6.25 us
    dot_general x16, matrix products, column_attention(): jnp.einsum('shd,thd->hst', queries, key_part, preferred_element_type=jnp....  5.03 us
    unnamed x19, local copies, waits for them, and re-layouts  4.99 us
  transfers between devices with their start and end apart: 2, of which 2 were waited for; matrix products, arithmetic and copies ran while one was open for 0% of the time, Pallas kernels for 0%

commit v1 on v0

--- a/solution.py
+++ b/solution.py
@@ -5,6 +5,29 @@
 
 HEADS = 8
 HEAD_DIM = 32
+
+
+def cut_along(array, dim, size):
+    dims = array.shape
+    blocks = array.reshape(*dims[:dim], size, dims[dim] // size, *dims[dim + 1 :])
+    return jnp.moveaxis(blocks, dim, 0)
+
+
+def in_order(blocks, dim):
+    shape = list(blocks.shape[1:])
+    shape[dim] *= blocks.shape[0]
+    return jnp.moveaxis(blocks, 0, dim).reshape(shape)
+
+
+def swapped_with_each(x, axis, split_dim, concat_dim):
+    size, index = (lax.axis_size(axis), lax.axis_index(axis))
+    tiles = cut_along(x, split_dim, size)
+    gathered = [tiles[index]]
+    for hop in range(1, size):
+        sent = tiles[index ^ hop]
+        gathered.append(lax.ppermute(sent, axis, [(i, i ^ hop) for i in range(size)]))
+    tiles = jnp.stack(gathered)[index ^ jnp.arange(size)]
+    return in_order(tiles, concat_dim)
 
 
 def normalize(values, gain):
@@ -48,7 +71,7 @@
     local_rows, single_block, segment, features = alignment.shape
     seq_devices = lax.axis_size("seq")
     split_view = alignment.reshape(local_rows, seq_devices, segment // seq_devices, features)
-    column_block = lax.all_to_all(split_view, "seq", split_axis=1, concat_axis=0, tiled=True)
+    column_block = swapped_with_each(split_view, "seq", 1, 0)
     seq_total, single, col_count, features = column_block.shape
     by_column = jnp.transpose(column_block.reshape(seq_total, col_count, features), (1, 0, 2))
     flat_rows = by_column.reshape(col_count * seq_total, features)

time: 153 us -> 152 us (level)
  the two profiles are of different devices: /device:TPU:12 before, /device:TPU:0 now
where the time goes in v1:
time: 152 us; the launch traced here: 151 us
  blocking collectives  43.6 us (29%)
  local copies, waits for them, and re-layouts  41.3 us (27%)
  waiting for transfers between devices  24.7 us (16%)
  starting transfers between devices  16.4 us (11%)
  matrix products  12 us (8%)
  other arithmetic  7.06 us (5%)
  between operations  5.3 us (3%)
    psum x1, blocking collectives, on_device(): loss_sum, mask_count = lax.psum((local_loss, local_count), ('seq', 'res'))  43.6 us
    squeeze x16, local copies, waits for them, and re-layouts, on_device(): lax.map(per_column, projected).reshape(col_count * seq_total, features)  15.5 us
    all_to_all x1, waiting for transfers between devices, on_device(): lax.all_to_all(result, 'res', split_axis=0, concat_axis=1, tiled=True)  13.3 us
    ppermute x7, starting transfers between devices, swapped_with_each(): lax.ppermute(sent, axis, [(i, i ^ hop) for i in range(size)])  12.7 us
    ppermute x7, waiting for transfers between devices, swapped_with_each(): lax.ppermute(sent, axis, [(i, i ^ hop) for i in range(size)])  11.4 us
    unnamed x30, local copies, waits for them, and re-layouts  8.42 us
    convert_element_type x1, local copies, waits for them, and re-layouts, project(): return jnp.dot(normed, w_proj.reshape(features, 4 * features), preferred_...  6.52 us
    dot_general x16, matrix products, column_attention(): jnp.einsum('shd,thd->hst', queries, key_part, preferred_element_type=jnp....  5.03 us
  transfers between devices with their start and end apart: 8, of which 2 were waited for; matrix products, arithmetic and copies ran while one was open for 3% of the time, Pallas kernels for 0%

profile of v1, /device:TPU:0, one launch (start us, length us, event | category | flops | bytes accessed | tf_op | source)
XLA Modules:
  0.0 151.1 jit_solution(11655106436328575513)
XLA Ops:
  0.7 1.4 dynamic-slice_bitcast_fusion.1
  2.1 3.0 %collective-permute-start = (bf16[16,1,16,256]{3,2,0,1:T(8,128)(2,1)S(1)}, bf16[16,1,16,256]{3,2,0,1:T(8,128)(2,1)}, u32[]{:S(2)}, u32[]{:S(2)}) collective-permute-start(bf16[16,1,16,256]{3,2,0,1:T(8,128)(2,1)S(1)} %get-tuple-element.68), channel_id=1, source_target_pairs={{0,4},{4,0},{8,12},{12,8},{16,20},{20,16},{24,28},{28,24},{1,5},{5... | collective-permute-start | bytes 393224 | tf_op jit(solution)/shard_map/ppermute | solution.py:28
  5.1 1.6 %collective-permute-start.1 = (bf16[16,1,16,256]{3,2,0,1:T(8,128)(2,1)S(1)}, bf16[16,1,16,256]{3,2,0,1:T(8,128)(2,1)}, u32[]{:S(2)}, u32[]{:S(2)}) collective-permute-start(bf16[16,1,16,256]{3,2,0,1:T(8,128)(2,1)S(1)} %get-tuple-element.67), channel_id=1, source_target_pairs={{0,8},{4,12},{8,0},{12,4},{16,24},{20,28},{24,16},{28,20},{1,9},{5... | collective-permute-start | bytes 393224 | tf_op jit(solution)/shard_map/ppermute | solution.py:28
  6.7 3.0 %collective-permute-start.3 = (bf16[16,1,16,256]{3,2,0,1:T(8,128)(2,1)S(1)}, bf16[16,1,16,256]{3,2,0,1:T(8,128)(2,1)S(1)}, u32[]{:S(2)}, u32[]{:S(2)}) collective-permute-start(bf16[16,1,16,256]{3,2,0,1:T(8,128)(2,1)S(1)} %get-tuple-element.65), channel_id=1, source_target_pairs={{0,16},{4,20},{8,24},{12,28},{16,0},{20,4},{24,8},{28,12},{1,17},{... | collective-permute-start | bytes 393224 | tf_op jit(solution)/shard_map/ppermute | solution.py:28
  9.7 1.3 collective-permute-start.4
  12.1 3.7 %collective-permute-start.5 = (bf16[16,1,16,256]{3,2,0,1:T(8,128)(2,1)S(1)}, bf16[16,1,16,256]{3,2,0,1:T(8,128)(2,1)S(1)}, u32[]{:S(2)}, u32[]{:S(2)}) collective-permute-start(bf16[16,1,16,256]{3,2,0,1:T(8,128)(2,1)S(1)} %get-tuple-element.63), channel_id=1, source_target_pairs={{0,24},{4,28},{8,16},{12,20},{16,8},{20,12},{24,0},{28,4},{1,25},{... | collective-permute-start | bytes 393224 | tf_op jit(solution)/shard_map/ppermute | solution.py:28
  17.8 11.4 %collective-permute-done.4 = bf16[16,1,16,256]{3,2,0,1:T(8,128)(2,1)S(1)} collective-permute-done((bf16[16,1,16,256]{3,2,0,1:T(8,128)(2,1)S(1)}, bf16[16,1,16,256]{3,2,0,1:T(8,128)(2,1)S(1)}, u32[]{:S(2)}, u32[]{:S(2)}) %collective-permute-start.4) | collective-permute-done | bytes 131104 | tf_op jit(solution)/shard_map/ppermute | solution.py:28
  30.2 1.2 bitcast_reduce_fusion
  31.3 1.2 copy.79
  32.6 1.6 %multiply_reduce_fusion.1 = f32[16,128]{1,0:T(8,128)S(1)} fusion(f32[16,128]{1,0:T(8,128)S(1)} %broadcast_multiply_fusion.1, f32[128,16,256]{2,1,0:T(8,128)S(1)} %bitcast_convert_fusion), kind=kLoop, calls=%fused_computation.25 | loop fusion | flops 1570816 | bytes 2113536 | tf_op jit(solution)/shard_map/reduce_sum | solution.py:36
  34.2 1.4 multiply_convert_fusion
  35.6 3.2 %convolution_convert_fusion = bf16[2048,1024]{1,0:T(8,128)(2,1)} fusion(bf16[2048,256]{1,0:T(8,128)(2,1)S(1)} %bitcast.151, bf16[256,1024]{1,0:T(8,128)(2,1)S(1)} %bitcast.153), kind=kOutput, calls=%fused_computation.13 | convolution fusion | flops 1075838976 | bytes 5767168 | tf_op jit(solution)/shard_map/dot_general | solution.py:43
  38.8 6.5 %copy.80 = bf16[2048,1024]{0,1:T(8,128)(2,1)} copy(bf16[2048,1024]{1,0:T(8,128)(2,1)} %convolution_convert_fusion) | data formatting | bytes 8388608 | tf_op jit(solution)/shard_map/convert_element_type | solution.py:45
  45.3 3.6 %copy.105 = bf16[128,8,16,128]{3,2,1,0:T(8,128)(2,1)S(1)} copy(bf16[128,8,16,128]{3,1,2,0:T(8,128)(2,1)} %bitcast.148) | data formatting | bytes 8388608
  48.9 3.0 %copy.81 = bf16[16,128,4,8,32]{1,4,3,2,0:T(8,128)(2,1)} copy(bf16[16,128,4,8,32]{1,0,4,3,2:T(8,128)(2,1)S(1)} %bitcast.149) | data formatting | bytes 8388608 | tf_op jit(solution)/shard_map/while | solution.py:88
  51.9 26.1 %while.10 = (s32[]{:T(128)}, bf16[16,128,256]{2,1,0:T(8,128)(2,1)S(1)}, bf16[16,128,4,8,32]{1,4,3,2,0:T(8,128)(2,1)}, s32[]{:T(128)}) while((s32[]{:T(128)}, bf16[16,128,256]{2,1,0:T(8,128)(2,1)S(1)}, bf16[16,128,4,8,32]{1,4,3,2,0:T(8,128)(2,1)}, s32[]{:T(128)}) %tuple.46), condition=%wide.region_4.0_spmd, body=%wide.region_2.4_spmd.sunk | while | flops 17398784 | bytes 1646653 | solution.py:88
  53.6 1.0 dynamic-slice_bitcast_fusion.9
  55.2 1.0 dynamic-slice_bitcast_fusion.9
  56.8 1.0 dynamic-slice_bitcast_fusion.9
  58.5 1.0 dynamic-slice_bitcast_fusion.9
  60.1 1.0 dynamic-slice_bitcast_fusion.9
  61.7 1.0 dynamic-slice_bitcast_fusion.9
  63.4 1.0 dynamic-slice_bitcast_fusion.9
  65.0 1.0 dynamic-slice_bitcast_fusion.9
  66.6 1.0 dynamic-slice_bitcast_fusion.9
  68.3 1.0 dynamic-slice_bitcast_fusion.9
  73.2 1.0 dynamic-slice_bitcast_fusion.9
  78.5 1.6 %copy.110 = bf16[16,128,256]{2,0,1:T(8,128)(2,1)} copy(bf16[16,128,256]{2,1,0:T(8,128)(2,1)S(1)} %bitcast.152) | data formatting | bytes 2097152 | tf_op jit(solution)/shard_map/reshape | solution.py:89
  80.1 3.7 %all-to-all-start = ((bf16[128,1,16,256]{3,2,1,0:T(8,128)(2,1)}), bf16[128,1,16,256]{3,2,1,0:T(8,128)(2,1)S(1)}, u32[]{:S(2)}, u32[]{:S(2)}) async-start(bf16[128,1,16,256]{3,2,1,0:T(8,128)(2,1)} %bitcast.125), calls=%async_computation | async-start | bytes 2097152 | tf_op jit(solution)/shard_map/all_to_all | solution.py:91
  84.7 13.3 %all-to-all-done = bf16[128,1,16,256]{3,2,1,0:T(8,128)(2,1)S(1)} async-done(((bf16[128,1,16,256]{3,2,1,0:T(8,128)(2,1)}), bf16[128,1,16,256]{3,2,1,0:T(8,128)(2,1)S(1)}, u32[]{:S(2)}, u32[]{:S(2)}) %all-to-all-start) | async-done | bytes 1048608 | tf_op jit(solution)/shard_map/all_to_all | solution.py:91
  102.1 43.6 %all-reduce = (f32[]{:T(128)}, f32[]{:T(128)}) all-reduce(f32[]{:T(128)} %get-tuple-element.51, f32[]{:T(128)} %get-tuple-element.50), channel_id=1, replica_groups=mesh['seq'=8,'res'=4] {'seq','res'}, use_global_device_ids=true, to_apply=%region_10.11 | all-reduce | flops 2 | bytes 16 | tf_op jit(solution)/shard_map/psum | solution.py:101
  147.0 1.1 copy.92
  (132 shorter events, 24.1 us)
Async XLA Ops:
  0.6 77.4 %copy-start = (bf16[256,256]{1,0:T(8,128)(2,1)S(1)}, bf16[256,256]{1,0:T(8,128)(2,1)}, u32[]{:S(2)}) copy-start(bf16[256,256]{1,0:T(8,128)(2,1)} %param.13) | copy-start | bytes 393220
  0.6 10.4 %copy-start.2 = (bf16[256,4,256]{2,1,0:T(4,128)(2,1)S(1)}, bf16[256,4,256]{2,1,0:T(4,128)(2,1)}, u32[]{:S(2)}) copy-start(bf16[256,4,256]{2,1,0:T(4,128)(2,1)} %param.12) | copy-start | bytes 1572868
  2.1 9.9 %collective-permute-start = (bf16[16,1,16,256]{3,2,0,1:T(8,128)(2,1)S(1)}, bf16[16,1,16,256]{3,2,0,1:T(8,128)(2,1)}, u32[]{:S(2)}, u32[]{:S(2)}) collective-permute-start(bf16[16,1,16,256]{3,2,0,1:T(8,128)(2,1)S(1)} %get-tuple-element.68), channel_id=1, source_target_pairs={{0,4},{4,0},{8,12},{12,8},{16,20},{20,16},{24,28},{28,24},{1,5},{5... | collective-permute-start | bytes 393224 | tf_op jit(solution)/shard_map/ppermute | solution.py:28
  5.1 11.5 %collective-permute-start.1 = (bf16[16,1,16,256]{3,2,0,1:T(8,128)(2,1)S(1)}, bf16[16,1,16,256]{3,2,0,1:T(8,128)(2,1)}, u32[]{:S(2)}, u32[]{:S(2)}) collective-permute-start(bf16[16,1,16,256]{3,2,0,1:T(8,128)(2,1)S(1)} %get-tuple-element.67), channel_id=1, source_target_pairs={{0,8},{4,12},{8,0},{12,4},{16,24},{20,28},{24,16},{28,20},{1,9},{5... | collective-permute-start | bytes 393224 | tf_op jit(solution)/shard_map/ppermute | solution.py:28
  6.7 11.0 %collective-permute-start.2 = (bf16[16,1,16,256]{3,2,0,1:T(8,128)(2,1)S(1)}, bf16[16,1,16,256]{3,2,0,1:T(8,128)(2,1)S(1)}, u32[]{:S(2)}, u32[]{:S(2)}) collective-permute-start(bf16[16,1,16,256]{3,2,0,1:T(8,128)(2,1)S(1)} %get-tuple-element.66), channel_id=1, source_target_pairs={{0,12},{4,8},{8,4},{12,0},{16,28},{20,24},{24,20},{28,16},{1,13},{... | collective-permute-start | bytes 393224 | tf_op jit(solution)/shard_map/ppermute | solution.py:28
  6.7 11.0 %collective-permute-start.3 = (bf16[16,1,16,256]{3,2,0,1:T(8,128)(2,1)S(1)}, bf16[16,1,16,256]{3,2,0,1:T(8,128)(2,1)S(1)}, u32[]{:S(2)}, u32[]{:S(2)}) collective-permute-start(bf16[16,1,16,256]{3,2,0,1:T(8,128)(2,1)S(1)} %get-tuple-element.65), channel_id=1, source_target_pairs={{0,16},{4,20},{8,24},{12,28},{16,0},{20,4},{24,8},{28,12},{1,17},{... | collective-permute-start | bytes 393224 | tf_op jit(solution)/shard_map/ppermute | solution.py:28
  9.7 19.4 %collective-permute-start.4 = (bf16[16,1,16,256]{3,2,0,1:T(8,128)(2,1)S(1)}, bf16[16,1,16,256]{3,2,0,1:T(8,128)(2,1)S(1)}, u32[]{:S(2)}, u32[]{:S(2)}) collective-permute-start(bf16[16,1,16,256]{3,2,0,1:T(8,128)(2,1)S(1)} %get-tuple-element.64), channel_id=1, source_target_pairs={{0,20},{4,16},{8,28},{12,24},{16,4},{20,0},{24,12},{28,8},{1,21},{... | collective-permute-start | bytes 393224 | tf_op jit(solution)/shard_map/ppermute | solution.py:28
  12.1 17.1 %collective-permute-start.5 = (bf16[16,1,16,256]{3,2,0,1:T(8,128)(2,1)S(1)}, bf16[16,1,16,256]{3,2,0,1:T(8,128)(2,1)S(1)}, u32[]{:S(2)}, u32[]{:S(2)}) collective-permute-start(bf16[16,1,16,256]{3,2,0,1:T(8,128)(2,1)S(1)} %get-tuple-element.63), channel_id=1, source_target_pairs={{0,24},{4,28},{8,16},{12,20},{16,8},{20,12},{24,0},{28,4},{1,25},{... | collective-permute-start | bytes 393224 | tf_op jit(solution)/shard_map/ppermute | solution.py:28
  16.7 12.5 %collective-permute-start.6 = (bf16[16,1,16,256]{3,2,0,1:T(8,128)(2,1)S(1)}, bf16[16,1,16,256]{3,2,0,1:T(8,128)(2,1)S(1)}, u32[]{:S(2)}, u32[]{:S(2)}) collective-permute-start(bf16[16,1,16,256]{3,2,0,1:T(8,128)(2,1)S(1)} %get-tuple-element.62), channel_id=1, source_target_pairs={{0,28},{4,24},{8,20},{12,16},{16,12},{20,8},{24,4},{28,0},{1,29},{... | collective-permute-start | bytes 393224 | tf_op jit(solution)/shard_map/ppermute | solution.py:28
  32.6 1.7 %copy-start.7 = (f32[256]{0:T(256)S(1)}, f32[256]{0:T(256)}, u32[]{:S(2)}) copy-start(f32[256]{0:T(256)} %param.11) | copy-start | bytes 3076
  48.9 3.0 %copy-start.1 = (bf16[16,128,256]{2,1,0:T(8,128)(2,1)S(1)}, bf16[16,128,256]{2,1,0:T(8,128)(2,1)}, u32[]{:S(2)}) copy-start(bf16[16,128,256]{2,1,0:T(8,128)(2,1)} %custom-call.3) | copy-start | bytes 3145732
  78.5 5.3 %copy-start.4 = (s32[32,4,16]{0,2,1:T(8,128)S(1)}, s32[32,4,16]{0,2,1:T(8,128)}, u32[]{:S(2)}) copy-start(s32[32,4,16]{0,2,1:T(8,128)} %param.17) | copy-start | bytes 24580
  78.5 5.5 %copy-start.5 = (s32[32,4,16]{0,2,1:T(8,128)S(1)}, s32[32,4,16]{0,2,1:T(8,128)}, u32[]{:S(2)}) copy-start(s32[32,4,16]{0,2,1:T(8,128)} %param.16) | copy-start | bytes 24580
  80.1 17.9 %all-to-all-start = ((bf16[128,1,16,256]{3,2,1,0:T(8,128)(2,1)}), bf16[128,1,16,256]{3,2,1,0:T(8,128)(2,1)S(1)}, u32[]{:S(2)}, u32[]{:S(2)}) async-start(bf16[128,1,16,256]{3,2,1,0:T(8,128)(2,1)} %bitcast.125), calls=%async_computation | async-start | bytes 2097152 | tf_op jit(solution)/shard_map/all_to_all | solution.py:91
  98.4 1.6 %copy-start.8 = (f32[256]{0:T(256)S(1)}, f32[256]{0:T(256)}, u32[]{:S(2)}) copy-start(f32[256]{0:T(256)} %param.14) | copy-start | bytes 3076
  99.0 2.0 %copy-start.6 = (bf16[256,23]{0,1:T(8,128)(2,1)S(1)}, bf16[256,23]{0,1:T(8,128)(2,1)}, u32[]{:S(2)}) copy-start(bf16[256,23]{0,1:T(8,128)(2,1)} %param.15) | copy-start | bytes 35332
  100.0 1.4 copy-start.3
